TPU v7x, 8 devices: a whole 2x2x1 slice. The times are simulated.
8 devices in a mesh: dp: 1 (over z), cols: 2 (over y), rows: 4 (over x, core).
Axes of the slice: x: 2, y: 2, z: 1, core: 2. Of those that a mesh axis runs over, the one named last changes fastest.
Arguments:
- h_init: bfloat16 [2, 128, 48, 128], P('dp', 'rows', 'cols')
- c_init: float32 [2, 128, 48, 128], P('dp', 'rows', 'cols')
- w_rec: bfloat16 [3, 3, 128, 512], replicated
- gate_bias: float32 [24, 512], replicated
Outputs:
- output 1: bfloat16 [24, 2, 128, 48, 128], P(None, 'dp', 'rows', 'cols')
- output 2: float32 [2, 128, 48, 128], P('dp', 'rows', 'cols')
All inputs are finite; a program needn't handle non-finite values.
Results may differ from a plain program's by a relative error of at most 0.00377757.
Values are sent between devices in bfloat16 or wider.
A program may use at most 1 GiB of HBM per device.

v0:
```python
import jax
import jax.numpy as jnp
from jax import lax
from jax.sharding import PartitionSpec as P


def lstm_update(gate_pre, c_prev):
    in_gate, forget_gate, out_gate, cand_gate = jnp.split(gate_pre, 4, axis=-1)
    c_next = jax.nn.sigmoid(forget_gate) * c_prev + jax.nn.sigmoid(in_gate) * jnp.tanh(cand_gate)
    h_next = (jax.nn.sigmoid(out_gate) * jnp.tanh(c_next)).astype(jnp.bfloat16)
    return h_next, c_next


def solution(mesh):
    row_count = mesh.shape["rows"]
    col_count = mesh.shape["cols"]
    rows_down = [(src_pos, src_pos + 1) for src_pos in range(row_count - 1)]
    rows_up = [(src_pos + 1, src_pos) for src_pos in range(row_count - 1)]
    cols_right = [(src_pos, src_pos + 1) for src_pos in range(col_count - 1)]
    cols_left = [(src_pos + 1, src_pos) for src_pos in range(col_count - 1)]

    def with_halo(tile):
        from_above = lax.ppermute(tile[:, -1:], "rows", rows_down)
        from_below = lax.ppermute(tile[:, :1], "rows", rows_up)
        tall_tile = jnp.concatenate([from_above, tile, from_below], axis=1)
        from_left = lax.ppermute(tall_tile[:, :, -1:], "cols", cols_right)
        from_right = lax.ppermute(tall_tile[:, :, :1], "cols", cols_left)
        return jnp.concatenate([from_left, tall_tile, from_right], axis=2)

    def device_fn(h_init, c_init, w_rec, gate_bias):
        def one_step(carry_in, bias_row):
            h_prev, c_prev = carry_in
            padded = with_halo(h_prev)
            gate_pre = lax.conv_general_dilated(padded, w_rec, (1, 1), "VALID", dimension_numbers=("NHWC", "HWIO", "NHWC"), preferred_element_type=jnp.float32) + bias_row
            h_next, c_next = lstm_update(gate_pre, c_prev)
            return (h_next, c_next), h_next

        final_state, h_seq = lax.scan(one_step, (h_init, c_init), gate_bias)
        return h_seq, final_state[1]

    state_spec = P("dp", "rows", "cols", None)
    return jax.shard_map(device_fn, mesh=mesh, in_specs=(state_spec, state_spec, P(), P()), out_specs=(P(None, "dp", "rows", "cols", None), state_spec), check_vma=False)
```

profile of v0, /device:TPU:0, one launch (start us, length us, event | category | flops | bytes accessed | tf_op | source)
XLA Modules:
  0.0 534.4 jit_solution(8791133820009273882)
XLA Ops:
  3.1 530.0 %while.14 = (s32[]{:T(128)}, bf16[2,32,24,128]{3,1,2,0:T(8,128)(2,1)S(1)}, f32[2,32,24,128]{3,1,2,0:T(8,128)S(1)}, bf16[24,2,32,24,128]{4,3,2,1,0:T(8,128)(2,1)}...) while((s32[]{:T(128)}, ...), condition=%wide.region_1.2_spmd, body=%wide.region_0.1_spmd.sunk | while | flops 2426298368 | bytes 29180240 | solution.py:38
  10.0 4.9 collective-permute-start.3
  31.4 4.5 collective-permute-start.3
  46.5 4.9 collective-permute-start.1
  68.6 4.9 collective-permute-start.1
  75.7 4.5 collective-permute-start.3
  90.8 4.9 collective-permute-start.1
  113.0 4.9 collective-permute-start.1
  120.1 4.5 collective-permute-start.3
  135.2 4.9 collective-permute-start.1
  142.3 4.5 collective-permute-start.3
  157.4 4.9 collective-permute-start.1
  179.5 4.9 collective-permute-start.1
  186.6 4.5 collective-permute-start.3
  201.7 4.9 collective-permute-start.1
  223.9 4.9 collective-permute-start.1
  246.1 4.9 collective-permute-start.1
  253.2 4.5 collective-permute-start.3
  268.3 4.9 collective-permute-start.1
  290.4 4.9 collective-permute-start.1
  297.5 4.5 collective-permute-start.3
  312.6 4.9 collective-permute-start.1
  319.7 4.5 collective-permute-start.3
  334.8 4.9 collective-permute-start.1
  357.0 4.9 collective-permute-start.1
  379.2 4.9 collective-permute-start.1
  401.4 4.9 collective-permute-start.1
  423.5 4.9 collective-permute-start.1
  445.7 4.9 collective-permute-start.1
  467.9 4.9 collective-permute-start.1
  490.1 4.9 collective-permute-start.1
  512.3 4.9 collective-permute-start.1
  (505 shorter events, 381.3 us)
Async XLA Ops:
  8.7 7.0 %collective-permute-start.2 = (bf16[2,34,1,128]{3,1,2,0:T(8,128)(2,1)S(1)}, bf16[2,34,1,128]{3,1,2,0:T(8,128)(2,1)S(1)}, u32[]{:S(2)}, u32[]{:S(2)}) collective-permute-start(bf16[2,34,1,128]{3,1,2,0:T(8,128)(2,1)S(1)} %get-tuple-element.114), channel_id=1, source_target_pairs={{4,0},{5,1},{6,2},{7,3}} | collective-permute-start | bytes 52232 | tf_op jit(solution)/shard_map/while/body/eval_jaxpr/ppermute | solution.py:27
  10.0 6.4 %collective-permute-start.3 = (bf16[2,34,1,128]{3,1,2,0:T(8,128)(2,1)S(1)}, bf16[2,34,1,128]{3,1,2,0:T(8,128)(2,1)S(1)}, u32[]{:S(2)}, u32[]{:S(2)}) collective-permute-start(bf16[2,34,1,128]{3,1,2,0:T(8,128)(2,1)S(1)} %get-tuple-element.115), channel_id=1, source_target_pairs={{0,4},{1,5},{2,6},{3,7}} | collective-permute-start | bytes 52232 | tf_op jit(solution)/shard_map/while/body/eval_jaxpr/ppermute | solution.py:26
  30.1 6.6 %collective-permute-start.2 = (bf16[2,34,1,128]{3,1,2,0:T(8,128)(2,1)S(1)}, bf16[2,34,1,128]{3,1,2,0:T(8,128)(2,1)S(1)}, u32[]{:S(2)}, u32[]{:S(2)}) collective-permute-start(bf16[2,34,1,128]{3,1,2,0:T(8,128)(2,1)S(1)} %get-tuple-element.114), channel_id=1, source_target_pairs={{4,0},{5,1},{6,2},{7,3}} | collective-permute-start | bytes 52232 | tf_op jit(solution)/shard_map/while/body/eval_jaxpr/ppermute | solution.py:27
  52.3 6.6 %collective-permute-start.2 = (bf16[2,34,1,128]{3,1,2,0:T(8,128)(2,1)S(1)}, bf16[2,34,1,128]{3,1,2,0:T(8,128)(2,1)S(1)}, u32[]{:S(2)}, u32[]{:S(2)}) collective-permute-start(bf16[2,34,1,128]{3,1,2,0:T(8,128)(2,1)S(1)} %get-tuple-element.114), channel_id=1, source_target_pairs={{4,0},{5,1},{6,2},{7,3}} | collective-permute-start | bytes 52232 | tf_op jit(solution)/shard_map/while/body/eval_jaxpr/ppermute | solution.py:27
  74.4 6.6 %collective-permute-start.2 = (bf16[2,34,1,128]{3,1,2,0:T(8,128)(2,1)S(1)}, bf16[2,34,1,128]{3,1,2,0:T(8,128)(2,1)S(1)}, u32[]{:S(2)}, u32[]{:S(2)}) collective-permute-start(bf16[2,34,1,128]{3,1,2,0:T(8,128)(2,1)S(1)} %get-tuple-element.114), channel_id=1, source_target_pairs={{4,0},{5,1},{6,2},{7,3}} | collective-permute-start | bytes 52232 | tf_op jit(solution)/shard_map/while/body/eval_jaxpr/ppermute | solution.py:27
  89.5 6.2 %collective-permute-start = (bf16[2,1,24,128]{3,1,2,0:T(2,128)(2,1)S(1)}, bf16[2,1,24,128]{3,1,2,0:T(2,128)(2,1)S(1)}, u32[]{:S(2)}, u32[]{:S(2)}) collective-permute-start(bf16[2,1,24,128]{3,1,2,0:T(2,128)(2,1)S(1)} %get-tuple-element.112), channel_id=1, source_target_pairs={{1,0},{2,1},{3,2},{5,4},{6,5},{7,6}} | collective-permute-start | bytes 36872 | tf_op jit(solution)/shard_map/while/body/eval_jaxpr/ppermute | solution.py:24
  96.6 6.6 %collective-permute-start.2 = (bf16[2,34,1,128]{3,1,2,0:T(8,128)(2,1)S(1)}, bf16[2,34,1,128]{3,1,2,0:T(8,128)(2,1)S(1)}, u32[]{:S(2)}, u32[]{:S(2)}) collective-permute-start(bf16[2,34,1,128]{3,1,2,0:T(8,128)(2,1)S(1)} %get-tuple-element.114), channel_id=1, source_target_pairs={{4,0},{5,1},{6,2},{7,3}} | collective-permute-start | bytes 52232 | tf_op jit(solution)/shard_map/while/body/eval_jaxpr/ppermute | solution.py:27
  118.8 6.6 %collective-permute-start.2 = (bf16[2,34,1,128]{3,1,2,0:T(8,128)(2,1)S(1)}, bf16[2,34,1,128]{3,1,2,0:T(8,128)(2,1)S(1)}, u32[]{:S(2)}, u32[]{:S(2)}) collective-permute-start(bf16[2,34,1,128]{3,1,2,0:T(8,128)(2,1)S(1)} %get-tuple-element.114), channel_id=1, source_target_pairs={{4,0},{5,1},{6,2},{7,3}} | collective-permute-start | bytes 52232 | tf_op jit(solution)/shard_map/while/body/eval_jaxpr/ppermute | solution.py:27
  141.0 6.6 %collective-permute-start.2 = (bf16[2,34,1,128]{3,1,2,0:T(8,128)(2,1)S(1)}, bf16[2,34,1,128]{3,1,2,0:T(8,128)(2,1)S(1)}, u32[]{:S(2)}, u32[]{:S(2)}) collective-permute-start(bf16[2,34,1,128]{3,1,2,0:T(8,128)(2,1)S(1)} %get-tuple-element.114), channel_id=1, source_target_pairs={{4,0},{5,1},{6,2},{7,3}} | collective-permute-start | bytes 52232 | tf_op jit(solution)/shard_map/while/body/eval_jaxpr/ppermute | solution.py:27
  156.1 6.2 %collective-permute-start = (bf16[2,1,24,128]{3,1,2,0:T(2,128)(2,1)S(1)}, bf16[2,1,24,128]{3,1,2,0:T(2,128)(2,1)S(1)}, u32[]{:S(2)}, u32[]{:S(2)}) collective-permute-start(bf16[2,1,24,128]{3,1,2,0:T(2,128)(2,1)S(1)} %get-tuple-element.112), channel_id=1, source_target_pairs={{1,0},{2,1},{3,2},{5,4},{6,5},{7,6}} | collective-permute-start | bytes 36872 | tf_op jit(solution)/shard_map/while/body/eval_jaxpr/ppermute | solution.py:24
  163.2 6.6 %collective-permute-start.2 = (bf16[2,34,1,128]{3,1,2,0:T(8,128)(2,1)S(1)}, bf16[2,34,1,128]{3,1,2,0:T(8,128)(2,1)S(1)}, u32[]{:S(2)}, u32[]{:S(2)}) collective-permute-start(bf16[2,34,1,128]{3,1,2,0:T(8,128)(2,1)S(1)} %get-tuple-element.114), channel_id=1, source_target_pairs={{4,0},{5,1},{6,2},{7,3}} | collective-permute-start | bytes 52232 | tf_op jit(solution)/shard_map/while/body/eval_jaxpr/ppermute | solution.py:27
  185.3 6.6 %collective-permute-start.2 = (bf16[2,34,1,128]{3,1,2,0:T(8,128)(2,1)S(1)}, bf16[2,34,1,128]{3,1,2,0:T(8,128)(2,1)S(1)}, u32[]{:S(2)}, u32[]{:S(2)}) collective-permute-start(bf16[2,34,1,128]{3,1,2,0:T(8,128)(2,1)S(1)} %get-tuple-element.114), channel_id=1, source_target_pairs={{4,0},{5,1},{6,2},{7,3}} | collective-permute-start | bytes 52232 | tf_op jit(solution)/shard_map/while/body/eval_jaxpr/ppermute | solution.py:27
  207.5 6.6 %collective-permute-start.2 = (bf16[2,34,1,128]{3,1,2,0:T(8,128)(2,1)S(1)}, bf16[2,34,1,128]{3,1,2,0:T(8,128)(2,1)S(1)}, u32[]{:S(2)}, u32[]{:S(2)}) collective-permute-start(bf16[2,34,1,128]{3,1,2,0:T(8,128)(2,1)S(1)} %get-tuple-element.114), channel_id=1, source_target_pairs={{4,0},{5,1},{6,2},{7,3}} | collective-permute-start | bytes 52232 | tf_op jit(solution)/shard_map/while/body/eval_jaxpr/ppermute | solution.py:27
  222.6 6.2 %collective-permute-start = (bf16[2,1,24,128]{3,1,2,0:T(2,128)(2,1)S(1)}, bf16[2,1,24,128]{3,1,2,0:T(2,128)(2,1)S(1)}, u32[]{:S(2)}, u32[]{:S(2)}) collective-permute-start(bf16[2,1,24,128]{3,1,2,0:T(2,128)(2,1)S(1)} %get-tuple-element.112), channel_id=1, source_target_pairs={{1,0},{2,1},{3,2},{5,4},{6,5},{7,6}} | collective-permute-start | bytes 36872 | tf_op jit(solution)/shard_map/while/body/eval_jaxpr/ppermute | solution.py:24
  229.7 6.6 %collective-permute-start.2 = (bf16[2,34,1,128]{3,1,2,0:T(8,128)(2,1)S(1)}, bf16[2,34,1,128]{3,1,2,0:T(8,128)(2,1)S(1)}, u32[]{:S(2)}, u32[]{:S(2)}) collective-permute-start(bf16[2,34,1,128]{3,1,2,0:T(8,128)(2,1)S(1)} %get-tuple-element.114), channel_id=1, source_target_pairs={{4,0},{5,1},{6,2},{7,3}} | collective-permute-start | bytes 52232 | tf_op jit(solution)/shard_map/while/body/eval_jaxpr/ppermute | solution.py:27
  251.9 6.6 %collective-permute-start.2 = (bf16[2,34,1,128]{3,1,2,0:T(8,128)(2,1)S(1)}, bf16[2,34,1,128]{3,1,2,0:T(8,128)(2,1)S(1)}, u32[]{:S(2)}, u32[]{:S(2)}) collective-permute-start(bf16[2,34,1,128]{3,1,2,0:T(8,128)(2,1)S(1)} %get-tuple-element.114), channel_id=1, source_target_pairs={{4,0},{5,1},{6,2},{7,3}} | collective-permute-start | bytes 52232 | tf_op jit(solution)/shard_map/while/body/eval_jaxpr/ppermute | solution.py:27
  267.0 6.2 %collective-permute-start = (bf16[2,1,24,128]{3,1,2,0:T(2,128)(2,1)S(1)}, bf16[2,1,24,128]{3,1,2,0:T(2,128)(2,1)S(1)}, u32[]{:S(2)}, u32[]{:S(2)}) collective-permute-start(bf16[2,1,24,128]{3,1,2,0:T(2,128)(2,1)S(1)} %get-tuple-element.112), channel_id=1, source_target_pairs={{1,0},{2,1},{3,2},{5,4},{6,5},{7,6}} | collective-permute-start | bytes 36872 | tf_op jit(solution)/shard_map/while/body/eval_jaxpr/ppermute | solution.py:24
  274.1 6.6 %collective-permute-start.2 = (bf16[2,34,1,128]{3,1,2,0:T(8,128)(2,1)S(1)}, bf16[2,34,1,128]{3,1,2,0:T(8,128)(2,1)S(1)}, u32[]{:S(2)}, u32[]{:S(2)}) collective-permute-start(bf16[2,34,1,128]{3,1,2,0:T(8,128)(2,1)S(1)} %get-tuple-element.114), channel_id=1, source_target_pairs={{4,0},{5,1},{6,2},{7,3}} | collective-permute-start | bytes 52232 | tf_op jit(solution)/shard_map/while/body/eval_jaxpr/ppermute | solution.py:27
  289.1 6.2 %collective-permute-start = (bf16[2,1,24,128]{3,1,2,0:T(2,128)(2,1)S(1)}, bf16[2,1,24,128]{3,1,2,0:T(2,128)(2,1)S(1)}, u32[]{:S(2)}, u32[]{:S(2)}) collective-permute-start(bf16[2,1,24,128]{3,1,2,0:T(2,128)(2,1)S(1)} %get-tuple-element.112), channel_id=1, source_target_pairs={{1,0},{2,1},{3,2},{5,4},{6,5},{7,6}} | collective-permute-start | bytes 36872 | tf_op jit(solution)/shard_map/while/body/eval_jaxpr/ppermute | solution.py:24
  296.2 6.6 %collective-permute-start.2 = (bf16[2,34,1,128]{3,1,2,0:T(8,128)(2,1)S(1)}, bf16[2,34,1,128]{3,1,2,0:T(8,128)(2,1)S(1)}, u32[]{:S(2)}, u32[]{:S(2)}) collective-permute-start(bf16[2,34,1,128]{3,1,2,0:T(8,128)(2,1)S(1)} %get-tuple-element.114), channel_id=1, source_target_pairs={{4,0},{5,1},{6,2},{7,3}} | collective-permute-start | bytes 52232 | tf_op jit(solution)/shard_map/while/body/eval_jaxpr/ppermute | solution.py:27
  318.4 6.6 %collective-permute-start.2 = (bf16[2,34,1,128]{3,1,2,0:T(8,128)(2,1)S(1)}, bf16[2,34,1,128]{3,1,2,0:T(8,128)(2,1)S(1)}, u32[]{:S(2)}, u32[]{:S(2)}) collective-permute-start(bf16[2,34,1,128]{3,1,2,0:T(8,128)(2,1)S(1)} %get-tuple-element.114), channel_id=1, source_target_pairs={{4,0},{5,1},{6,2},{7,3}} | collective-permute-start | bytes 52232 | tf_op jit(solution)/shard_map/while/body/eval_jaxpr/ppermute | solution.py:27
  333.5 6.2 %collective-permute-start = (bf16[2,1,24,128]{3,1,2,0:T(2,128)(2,1)S(1)}, bf16[2,1,24,128]{3,1,2,0:T(2,128)(2,1)S(1)}, u32[]{:S(2)}, u32[]{:S(2)}) collective-permute-start(bf16[2,1,24,128]{3,1,2,0:T(2,128)(2,1)S(1)} %get-tuple-element.112), channel_id=1, source_target_pairs={{1,0},{2,1},{3,2},{5,4},{6,5},{7,6}} | collective-permute-start | bytes 36872 | tf_op jit(solution)/shard_map/while/body/eval_jaxpr/ppermute | solution.py:24
  340.6 6.6 %collective-permute-start.2 = (bf16[2,34,1,128]{3,1,2,0:T(8,128)(2,1)S(1)}, bf16[2,34,1,128]{3,1,2,0:T(8,128)(2,1)S(1)}, u32[]{:S(2)}, u32[]{:S(2)}) collective-permute-start(bf16[2,34,1,128]{3,1,2,0:T(8,128)(2,1)S(1)} %get-tuple-element.114), channel_id=1, source_target_pairs={{4,0},{5,1},{6,2},{7,3}} | collective-permute-start | bytes 52232 | tf_op jit(solution)/shard_map/while/body/eval_jaxpr/ppermute | solution.py:27
  362.8 6.6 %collective-permute-start.2 = (bf16[2,34,1,128]{3,1,2,0:T(8,128)(2,1)S(1)}, bf16[2,34,1,128]{3,1,2,0:T(8,128)(2,1)S(1)}, u32[]{:S(2)}, u32[]{:S(2)}) collective-permute-start(bf16[2,34,1,128]{3,1,2,0:T(8,128)(2,1)S(1)} %get-tuple-element.114), channel_id=1, source_target_pairs={{4,0},{5,1},{6,2},{7,3}} | collective-permute-start | bytes 52232 | tf_op jit(solution)/shard_map/while/body/eval_jaxpr/ppermute | solution.py:27
  385.0 6.6 %collective-permute-start.2 = (bf16[2,34,1,128]{3,1,2,0:T(8,128)(2,1)S(1)}, bf16[2,34,1,128]{3,1,2,0:T(8,128)(2,1)S(1)}, u32[]{:S(2)}, u32[]{:S(2)}) collective-permute-start(bf16[2,34,1,128]{3,1,2,0:T(8,128)(2,1)S(1)} %get-tuple-element.114), channel_id=1, source_target_pairs={{4,0},{5,1},{6,2},{7,3}} | collective-permute-start | bytes 52232 | tf_op jit(solution)/shard_map/while/body/eval_jaxpr/ppermute | solution.py:27
  400.1 6.2 %collective-permute-start = (bf16[2,1,24,128]{3,1,2,0:T(2,128)(2,1)S(1)}, bf16[2,1,24,128]{3,1,2,0:T(2,128)(2,1)S(1)}, u32[]{:S(2)}, u32[]{:S(2)}) collective-permute-start(bf16[2,1,24,128]{3,1,2,0:T(2,128)(2,1)S(1)} %get-tuple-element.112), channel_id=1, source_target_pairs={{1,0},{2,1},{3,2},{5,4},{6,5},{7,6}} | collective-permute-start | bytes 36872 | tf_op jit(solution)/shard_map/while/body/eval_jaxpr/ppermute | solution.py:24
  407.2 6.6 %collective-permute-start.2 = (bf16[2,34,1,128]{3,1,2,0:T(8,128)(2,1)S(1)}, bf16[2,34,1,128]{3,1,2,0:T(8,128)(2,1)S(1)}, u32[]{:S(2)}, u32[]{:S(2)}) collective-permute-start(bf16[2,34,1,128]{3,1,2,0:T(8,128)(2,1)S(1)} %get-tuple-element.114), channel_id=1, source_target_pairs={{4,0},{5,1},{6,2},{7,3}} | collective-permute-start | bytes 52232 | tf_op jit(solution)/shard_map/while/body/eval_jaxpr/ppermute | solution.py:27
  429.3 6.6 %collective-permute-start.2 = (bf16[2,34,1,128]{3,1,2,0:T(8,128)(2,1)S(1)}, bf16[2,34,1,128]{3,1,2,0:T(8,128)(2,1)S(1)}, u32[]{:S(2)}, u32[]{:S(2)}) collective-permute-start(bf16[2,34,1,128]{3,1,2,0:T(8,128)(2,1)S(1)} %get-tuple-element.114), channel_id=1, source_target_pairs={{4,0},{5,1},{6,2},{7,3}} | collective-permute-start | bytes 52232 | tf_op jit(solution)/shard_map/while/body/eval_jaxpr/ppermute | solution.py:27
  451.5 6.6 %collective-permute-start.2 = (bf16[2,34,1,128]{3,1,2,0:T(8,128)(2,1)S(1)}, bf16[2,34,1,128]{3,1,2,0:T(8,128)(2,1)S(1)}, u32[]{:S(2)}, u32[]{:S(2)}) collective-permute-start(bf16[2,34,1,128]{3,1,2,0:T(8,128)(2,1)S(1)} %get-tuple-element.114), channel_id=1, source_target_pairs={{4,0},{5,1},{6,2},{7,3}} | collective-permute-start | bytes 52232 | tf_op jit(solution)/shard_map/while/body/eval_jaxpr/ppermute | solution.py:27
  473.7 6.6 %collective-permute-start.2 = (bf16[2,34,1,128]{3,1,2,0:T(8,128)(2,1)S(1)}, bf16[2,34,1,128]{3,1,2,0:T(8,128)(2,1)S(1)}, u32[]{:S(2)}, u32[]{:S(2)}) collective-permute-start(bf16[2,34,1,128]{3,1,2,0:T(8,128)(2,1)S(1)} %get-tuple-element.114), channel_id=1, source_target_pairs={{4,0},{5,1},{6,2},{7,3}} | collective-permute-start | bytes 52232 | tf_op jit(solution)/shard_map/while/body/eval_jaxpr/ppermute | solution.py:27
  495.9 6.6 %collective-permute-start.2 = (bf16[2,34,1,128]{3,1,2,0:T(8,128)(2,1)S(1)}, bf16[2,34,1,128]{3,1,2,0:T(8,128)(2,1)S(1)}, u32[]{:S(2)}, u32[]{:S(2)}) collective-permute-start(bf16[2,34,1,128]{3,1,2,0:T(8,128)(2,1)S(1)} %get-tuple-element.114), channel_id=1, source_target_pairs={{4,0},{5,1},{6,2},{7,3}} | collective-permute-start | bytes 52232 | tf_op jit(solution)/shard_map/while/body/eval_jaxpr/ppermute | solution.py:27
  518.1 6.6 %collective-permute-start.2 = (bf16[2,34,1,128]{3,1,2,0:T(8,128)(2,1)S(1)}, bf16[2,34,1,128]{3,1,2,0:T(8,128)(2,1)S(1)}, u32[]{:S(2)}, u32[]{:S(2)}) collective-permute-start(bf16[2,34,1,128]{3,1,2,0:T(8,128)(2,1)S(1)} %get-tuple-element.114), channel_id=1, source_target_pairs={{4,0},{5,1},{6,2},{7,3}} | collective-permute-start | bytes 52232 | tf_op jit(solution)/shard_map/while/body/eval_jaxpr/ppermute | solution.py:27
  (66 other events, 382.6 us)
where the time goes:
time: 542 us; the launch traced here: 534 us
  starting transfers between devices  287 us (53%)
  local copies, waits for them, and re-layouts  96.7 us (18%)
  matrix products  69.8 us (13%)
  other arithmetic  40.1 us (7%)
  waiting for transfers between devices  37.3 us (7%)
    ppermute x24, starting transfers between devices, with_halo(): from_above = lax.ppermute(tile[:, -1:], 'rows', rows_down)  116 us
    ppermute x24, starting transfers between devices, with_halo(): from_left = lax.ppermute(tall_tile[:, :, -1:], 'cols', cols_right)  109 us
    conv_general_dilated x24, matrix products, one_step(): lax.conv_general_dilated(padded, w_rec, (1, 1), 'VALID', dimension_number...  69.8 us
    ppermute x24, starting transfers between devices, with_halo(): from_below = lax.ppermute(tile[:, :1], 'rows', rows_up)  31 us
    ppermute x24, starting transfers between devices, with_halo(): from_right = lax.ppermute(tall_tile[:, :, :1], 'cols', cols_left)  31 us
    div x48, local copies, waits for them, and re-layouts, lstm_update(): jax.nn.sigmoid(forget_gate) * c_prev  29.4 us
    div x24, other arithmetic, lstm_update(): jax.nn.sigmoid(forget_gate) * c_prev  22.9 us
    dynamic_update_slice x24, local copies, waits for them, and re-layouts, device_fn(): final_state, h_seq = lax.scan(one_step, (h_init, c_init), gate_bias)  21.7 us
  transfers between devices with their start and end apart: 96, of which 48 were waited for; matrix products, arithmetic and copies ran while one was open for 3% of the time, Pallas kernels for 0%

commit v1 on v0

v1 whole, which is shorter than its diff:
```python
import jax
import jax.numpy as jnp
from jax import lax
from jax.experimental import pallas as pl
from jax.experimental.pallas import tpu as pltpu
from jax.sharding import PartitionSpec as P

MESH = pl.DeviceIdType.MESH
STEPS, BATCH, H, W, C = 24, 2, 32, 24, 128
RC = 8
NC = H // RC
M = RC * W
PITCH = 40
ROWS = H + 2


def sigmoid(x):
    return 0.5 * jnp.tanh(0.5 * x) + 0.5


def kernel(h0, c0, w, bias, hseq, clast, hxa, hxb, stage, sendcol, recvcol, recvcor, recvrow,
           s_col, r_col, s_cor, r_cor, s_row, r_row, s_out):
    hx = (hxa, hxb)
    row = lax.axis_index("rows")
    col = lax.axis_index("cols")
    nrow = lax.axis_size("rows")
    up = lax.rem(row + nrow - 1, nrow)
    down = lax.rem(row + 1, nrow)
    side = 1 - col
    dev_side = {"cols": side}
    dev_row = ({"rows": up}, {"rows": down})
    dev_cor = ({"rows": up, "cols": side}, {"rows": down, "cols": side})

    barrier = pltpu.get_barrier_semaphore()
    for dev in (dev_side,) + dev_row + dev_cor:
        pl.semaphore_signal(barrier, inc=1, device_id=dev, device_id_type=MESH)

    has = (jnp.where(row > 0, 1.0, 0.0), jnp.where(row < nrow - 1, 1.0, 0.0))
    is_left = jnp.where(col == 0, 1.0, 0.0)

    def col_copy(s, b, i):
        return pltpu.make_async_remote_copy(sendcol.at[s, b, i], recvcol.at[s, b, i], s_col.at[s, b, i], r_col.at[s, b, i],
                                            device_id=dev_side, device_id_type=MESH)

    def cor_copy(s, b, d):
        i = 0 if d == 0 else NC - 1
        return pltpu.make_async_remote_copy(sendcol.at[s, b, i], recvcor.at[s, b, 1 - d], s_cor.at[s, b, d], r_cor.at[s, b, 1 - d],
                                            device_id=dev_cor[d], device_id_type=MESH)

    def row_copy(s, b, d):
        src = 1 if d == 0 else H
        return pltpu.make_async_remote_copy(hx[s].at[b, src, 8:8 + W, :], recvrow.at[s, b, 1 - d], s_row.at[s, b, d],
                                            r_row.at[s, b, 1 - d], device_id=dev_row[d], device_id_type=MESH)

    def out_copy(s, b, t):
        return pltpu.make_async_copy(stage.at[s, b], hseq.at[t, b], s_out.at[s, b])

    def put(s, b, i, h, send):
        h3 = h.reshape(RC, W, C)
        hx[s][b, 1 + i * RC:1 + (i + 1) * RC, 8:8 + W, :] = h3
        if send:
            sendcol[s, b, i] = jnp.where(col == 0, h3[:, W - 1, :], h3[:, 0, :])
            col_copy(s, b, i).start()
            if i == 0:
                row_copy(s, b, 0).start()
                cor_copy(s, b, 0).start()
            if i == NC - 1:
                row_copy(s, b, 1).start()
                cor_copy(s, b, 1).start()

    def send_done(s, b, i):
        col_copy(s, b, i).wait_send()
        if i == 0:
            row_copy(s, b, 0).wait_send()
            cor_copy(s, b, 0).wait_send()
        if i == NC - 1:
            row_copy(s, b, 1).wait_send()
            cor_copy(s, b, 1).wait_send()

    def take_col(s, b, i):
        col_copy(s, b, i).wait_recv()
        v = recvcol[s, b, i]
        hx[s][b, 1 + i * RC:1 + (i + 1) * RC, 7, :] = v * (1.0 - is_left)
        hx[s][b, 1 + i * RC:1 + (i + 1) * RC, 8 + W, :] = v * is_left

    def take_row(s, b, d):
        r = 0 if d == 0 else H + 1
        k = RC - 1 if d == 0 else 0
        row_copy(s, b, 1 - d).wait_recv()
        cor_copy(s, b, 1 - d).wait_recv()
        hx[s][b, r, 8:8 + W, :] = recvrow[s, b, d] * has[d]
        v = recvcor[s, b, d, k:k + 1, :] * has[d]
        hx[s][b, r, 7:8, :] = v * (1.0 - is_left)
        hx[s][b, r, 8 + W:9 + W, :] = v * is_left

    def step(s, t, send, first_out):
        n = 1 - s
        bias_row = bias[pl.ds(t, 1), :]
        for b in range(BATCH):
            for i in range(NC):
                if i == 0:
                    take_col(s, b, 0)
                    take_row(s, b, 0)
                if i + 1 < NC:
                    take_col(s, b, i + 1)
                else:
                    take_row(s, b, 1)
                taps = []
                for dh in range(3):
                    for dw in range(3):
                        v = hx[s][b, i * RC + dh:(i + 1) * RC + dh, 7 + dw:7 + dw + W, :]
                        taps.append(v.reshape(M, C).astype(jnp.bfloat16))
                lhs = jnp.concatenate(taps, axis=1)
                gate = jnp.dot(lhs, w[...], preferred_element_type=jnp.float32) + bias_row
                c_prev = clast[b, i * M:(i + 1) * M, :]
                c_next = (sigmoid(gate[:, C:2 * C]) * c_prev
                          + sigmoid(gate[:, :C]) * jnp.tanh(gate[:, 3 * C:]))
                clast[b, i * M:(i + 1) * M, :] = c_next
                h = (sigmoid(gate[:, 2 * C:3 * C]) * jnp.tanh(c_next)).astype(jnp.bfloat16)
                stage[n, b, i * M:(i + 1) * M, :] = h
                send_done(s, b, i)
                put(n, b, i, h.astype(jnp.float32), send)
            if not first_out:
                out_copy(s, b, t - 1).wait()
            out_copy(n, b, t).start()

    clast[...] = c0[...]
    for s in range(2):
        for b in range(BATCH):
            hx[s][b, :, 0:8, :] = jnp.zeros((ROWS, 8, C), jnp.float32)
            hx[s][b, :, 8 + W:PITCH, :] = jnp.zeros((ROWS, PITCH - 8 - W, C), jnp.float32)
    pl.semaphore_wait(barrier, 5)
    for b in range(BATCH):
        for i in range(NC):
            put(0, b, i, h0[b, i * M:(i + 1) * M, :].astype(jnp.float32), True)

    step(0, 0, True, True)
    step(1, 1, True, False)

    def pair(p, _):
        step(0, 2 * p, True, False)
        step(1, 2 * p + 1, True, False)
        return 0

    lax.fori_loop(1, STEPS // 2 - 1, pair, 0)
    step(0, STEPS - 2, True, False)
    step(1, STEPS - 1, False, False)
    for b in range(BATCH):
        out_copy(0, b, STEPS - 1).wait()


def solution(mesh):
    def device_fn(h_init, c_init, w_rec, gate_bias):
        cells = H * W
        vm = pl.BlockSpec(memory_space=pltpu.VMEM)
        hseq, clast = pl.pallas_call(
            kernel,
            out_shape=(jax.ShapeDtypeStruct((STEPS, BATCH, cells, C), jnp.bfloat16),
                       jax.ShapeDtypeStruct((BATCH, cells, C), jnp.float32)),
            in_specs=[vm] * 4,
            out_specs=(pl.BlockSpec(memory_space=pl.ANY), vm),
            scratch_shapes=[
                pltpu.VMEM((BATCH, ROWS, PITCH, C), jnp.float32),
                pltpu.VMEM((BATCH, ROWS, PITCH, C), jnp.float32),
                pltpu.VMEM((2, BATCH, cells, C), jnp.bfloat16),
                pltpu.VMEM((2, BATCH, NC, RC, C), jnp.float32),
                pltpu.VMEM((2, BATCH, NC, RC, C), jnp.float32),
                pltpu.VMEM((2, BATCH, 2, RC, C), jnp.float32),
                pltpu.VMEM((2, BATCH, 2, W, C), jnp.float32),
                pltpu.SemaphoreType.DMA((2, BATCH, NC)),
                pltpu.SemaphoreType.DMA((2, BATCH, NC)),
                pltpu.SemaphoreType.DMA((2, BATCH, 2)),
                pltpu.SemaphoreType.DMA((2, BATCH, 2)),
                pltpu.SemaphoreType.DMA((2, BATCH, 2)),
                pltpu.SemaphoreType.DMA((2, BATCH, 2)),
                pltpu.SemaphoreType.DMA((2, BATCH)),
            ],
            compiler_params=pltpu.CompilerParams(collective_id=0, has_side_effects=True, vmem_limit_bytes=48 << 20),
        )(h_init.reshape(BATCH, cells, C), c_init.reshape(BATCH, cells, C), w_rec.reshape(9 * C, 4 * C), gate_bias)
        return hseq.reshape(STEPS, BATCH, H, W, C), clast.reshape(BATCH, H, W, C)

    state_spec = P("dp", "rows", "cols", None)
    return jax.shard_map(device_fn, mesh=mesh, in_specs=(state_spec, state_spec, P(), P()),
                         out_specs=(P(None, "dp", "rows", "cols", None), state_spec), check_vma=False)
```

time: 542 us -> 133 us (0.25); the launches traced: 534 us -> 133 us
  starting transfers between devices: 287 us -> 0 us
  Pallas kernels: 0 us -> 117 us
  local copies, waits for them, and re-layouts: 96.7 us -> 15.3 us
  matrix products: 69.8 us -> 0 us
  other arithmetic: 40.1 us -> 0 us
  waiting for transfers between devices: 37.3 us -> 0 us
    ppermute x96 -> x0, starting transfers between devices: 287 us -> none  [the longest x24 116 us: with_halo(): from_above = lax.ppermute(tile[:, -1:], 'rows', rows_down)]
    pallas_call x0 -> x1, Pallas kernels: none -> 117 us  [device_fn(): pl.pallas_call(kernel, out_shape=(jax.ShapeDtypeStruct((STEPS, BATCH, cel...]
    conv_general_dilated x24 -> x0, matrix products: 69.8 us -> none  [one_step(): lax.conv_general_dilated(padded, w_rec, (1, 1), 'VALID', dimension_number...]
    ppermute x96 -> x0, waiting for transfers between devices: 37.3 us -> none  [the longest x24 19.7 us: with_halo(): from_above = lax.ppermute(tile[:, -1:], 'rows', rows_down)]
    div x48 -> x0, local copies, waits for them, and re-layouts: 29.4 us -> none  [lstm_update(): jax.nn.sigmoid(forget_gate) * c_prev]
    div x24 -> x0, other arithmetic: 22.9 us -> none  [lstm_update(): jax.nn.sigmoid(forget_gate) * c_prev]
    dynamic_update_slice x24 -> x0, local copies, waits for them, and re-layouts: 21.7 us -> none  [device_fn(): final_state, h_seq = lax.scan(one_step, (h_init, c_init), gate_bias)]
    dynamic_slice x24 -> x0, local copies, waits for them, and re-layouts: 17.5 us -> none  [device_fn(): final_state, h_seq = lax.scan(one_step, (h_init, c_init), gate_bias)]
  transfers between devices with their start and end apart: 96 -> 0, of which waited for: 48 -> 0; matrix products, arithmetic and copies ran while one was open for 3% -> 0% of each run, Pallas kernels for 0% -> 0%
where the time goes in v1:
time: 133 us
  Pallas kernels  117 us (88%)
  local copies, waits for them, and re-layouts  15.3 us (12%)
    pallas_call x1, Pallas kernels, device_fn(): pl.pallas_call(kernel, out_shape=(jax.ShapeDtypeStruct((STEPS, BATCH, cel...  117 us
    unnamed x10, local copies, waits for them, and re-layouts  15.3 us

profile of v1, /device:TPU:0, one launch (start us, length us, event | category | flops | bytes accessed | tf_op | source)
XLA Modules:
  0.0 132.6 jit_solution(7285067164584581957)
XLA Ops:
  0.6 0.0 copy-start
  0.6 1.3 copy-done
  1.9 0.0 copy-start.1
  1.9 1.1 copy-done.1
  3.0 0.0 copy-start.2
  3.0 1.0 copy-done.2
  4.0 0.0 copy-start.3
  4.0 0.8 copy-done.3
  4.8 116.6 %shard_map.59 = (bf16[24,2,768,128]{3,2,1,0:T(8,128)(2,1)}, f32[2,768,128]{2,1,0:T(8,128)S(1)}) custom-call(bf16[2,768,128]{2,1,0:T(8,128)(2,1)S(1)} %bitcast.8, f32[2,768,128]{2,1,0:T(8,128)S(1)} %bitcast.7, bf16[1152,512]{1,0:T(8,128)(2,1)S(1)} %bitcast.5, f32[24,512]{1,0:T(8,128)S(1)} %copy-done.3), custom_call_target="tpu_custom_call" | custom-call | tf_op jit(solution)/shard_map/pallas_call | solution.py:156
  121.5 10.3 %copy.8 = bf16[24,2,32,24,128]{4,3,2,1,0:T(8,128)(2,1)} copy(bf16[24,2,32,24,128]{4,3,2,1,0:T(8,128)(2,1)} %bitcast.9) | data formatting | bytes 18874368
  131.7 0.9 copy.9
Async XLA Ops:
  0.6 1.3 copy-start
  1.9 1.1 copy-start.1
  3.0 1.0 copy-start.2
  4.0 0.8 copy-start.3

commit v2 on v0

v2 whole, which is shorter than its diff:
```python
import jax
import jax.numpy as jnp
from jax import lax
from jax.experimental import pallas as pl
from jax.experimental.pallas import tpu as pltpu
from jax.sharding import PartitionSpec as P

MESH = pl.DeviceIdType.MESH
STEPS, BATCH, H, W, C = 24, 2, 32, 24, 128
PERIODS = STEPS // 2
RC = 8
NC = H // RC
M = RC * W
PITCH = 40
PAD = 8
ROWS = H + 2 * PAD
SP = 16
SROWS = H + 2 * SP
A_ORDER = (1, 2, 0, 3)
B_ORDER = (1, 2, 0, 3)


def sigmoid(x):
    return 0.5 * jnp.tanh(0.5 * x) + 0.5


def kernel(h0, c0, w, bias, hseq, c, ha, hb, hodd, sa, sb, crow, rsend, csend, ssend, stage,
           s_col, r_col, s_row, r_row, s_crow, r_crow, s_own, r_own, s_cor, r_cor, s_out):
    he = (ha, hb)
    st = (sa, sb)
    row = lax.axis_index("rows")
    col = lax.axis_index("cols")
    nrow = lax.axis_size("rows")
    up = lax.rem(row + nrow - 1, nrow)
    down = lax.rem(row + 1, nrow)
    side = 1 - col
    dev_side = {"cols": side}
    dev_row = ({"rows": up}, {"rows": down})
    dev_cor = ({"rows": up, "cols": side}, {"rows": down, "cols": side})

    has = (row > 0, row < nrow - 1)
    halo_w = jnp.where(col == 0, 8 + W, 7)
    edge_w = jnp.where(col == 0, 7 + W, 8)
    next_w = jnp.where(col == 0, 6 + W, 9)
    edge_c = jnp.where(col == 0, W - 1, 0)
    tap_plane = (jnp.where(col == 0, 0, 4), 3, jnp.where(col == 0, 4, 0))

    def remote(src, dst, ssem, rsem, dev):
        return pltpu.make_async_remote_copy(src, dst, ssem, rsem, device_id=dev, device_id_type=MESH)

    def col_copy(s, b, i):
        rows = pl.ds(SP + i * RC, RC)
        return [remote(st[s].at[b, 0:3, rows, :], st[s].at[b, 3:6, rows, :], s_col.at[s, b, i], r_col.at[s, b, i], dev_side)]

    def row_copies(s, b, d):
        o = 1 - d
        rows = pl.ds(PAD + H if d == 0 else PAD - 2, 2)
        srows = pl.ds(SP + H if d == 0 else SP - RC, RC)
        return [
            remote(rsend.at[s, b, d], he[s].at[b, rows, 8:8 + W, :], s_row.at[s, b, d], r_row.at[s, b, o], dev_row[d]),
            remote(csend.at[s, b, d], crow.at[s, b, o], s_crow.at[s, b, d], r_crow.at[s, b, o], dev_row[d]),
            remote(ssend.at[s, b, d, 0:1], st[s].at[b, 0:1, srows, :], s_own.at[s, b, d], r_own.at[s, b, o], dev_row[d]),
            remote(ssend.at[s, b, d], st[s].at[b, 3:6, srows, :], s_cor.at[s, b, d], r_cor.at[s, b, o], dev_cor[d]),
        ]

    def flat(ref, b):
        return ref.at[b].reshape(ROWS * PITCH, C)

    def strided(start, stride):
        return pl.ds(start, RC, stride)

    def out_copy(k, b, t):
        return pltpu.make_async_copy(stage.at[k, b], hseq.at[t, b], s_out.at[k, b])

    def put(s, b, i, h3, c2, send):
        he[s][b, PAD + i * RC:PAD + (i + 1) * RC, 8:8 + W, :] = h3
        if not send:
            return
        f = flat(he[s], b)
        base = (PAD + i * RC) * PITCH
        strip = (f[strided(base + edge_w, PITCH), :], f[strided(base + next_w, PITCH), :],
                 c.at[b][strided(i * M + edge_c, W), :])
        for k in range(3):
            st[s][b, k, SP + i * RC:SP + (i + 1) * RC, :] = strip[k]
        col_copy(s, b, i)[0].start()
        for d in range(2):
            if i == (0 if d == 0 else NC - 1):
                r = 0 if d == 0 else RC - 2
                q = 0 if d == 0 else (RC - 1) * W
                rsend[s, b, d] = jnp.where(has[d], h3[r:r + 2], 0.0)
                csend[s, b, d] = jnp.where(has[d], c2[q:q + W], 0.0)
                for k in range(3):
                    ssend[s, b, d, k] = jnp.where(has[d], strip[k], 0.0)
                for cp in row_copies(s, b, d):
                    cp.start()

    def insert(s, b, i):
        flat(he[s], b)[strided((PAD + i * RC) * PITCH + halo_w, PITCH), :] = st[s][b, 3, SP + i * RC:SP + (i + 1) * RC, :]

    def take_col(s, b, i):
        cp = col_copy(s, b, i)[0]
        cp.wait_send()
        cp.wait_recv()
        insert(s, b, i)

    def take_row(s, b, d):
        for cp in row_copies(s, b, d):
            cp.wait_send()
        for cp in row_copies(s, b, 1 - d):
            cp.wait_recv()
        insert(s, b, -1 if d == 0 else NC)

    def gates(parts, t):
        lhs = jnp.concatenate(parts, axis=1)
        return jnp.dot(lhs, w[...], preferred_element_type=jnp.float32)

    def update(gate, t, c_prev):
        gate = gate + bias[pl.ds(t, 1), :]
        c_next = sigmoid(gate[:, C:2 * C]) * c_prev + sigmoid(gate[:, :C]) * jnp.tanh(gate[:, 3 * C:])
        return (sigmoid(gate[:, 2 * C:3 * C]) * jnp.tanh(c_next)).astype(jnp.bfloat16), c_next

    def unit_a(s, b, i, t, seen):
        lo = i * RC - (1 if i == 0 else 0)
        n = RC + (1 if i in (0, NC - 1) else 0)
        wlo = i * RC - (RC if i == 0 else 0)
        wn = RC * (2 if i in (0, NC - 1) else 1)

        def dot():
            for j in range(max(i - 1, 0), min(i + 2, NC)):
                if j not in seen:
                    seen.add(j)
                    take_col(s, b, j)
            if i == 0:
                take_row(s, b, 0)
            if i == NC - 1:
                take_row(s, b, 1)
            parts = []
            for dh in range(3):
                for dw in range(3):
                    v = he[s][b, PAD + lo + dh - 1:PAD + lo + dh - 1 + n, 7 + dw:7 + dw + W, :].reshape(n * W, C)
                    r = st[s][b, tap_plane[dw], SP + wlo + dh - 1:SP + wlo + dh - 1 + wn, :]
                    v = jnp.concatenate([v, r, jnp.zeros((8, C), jnp.float32)], axis=0)
                    parts.append(v.astype(jnp.bfloat16))
            return gates(parts, t)

        def epilogue(gate):
            cm = c[b, i * M:(i + 1) * M, :]
            cw = st[s][b, 5, SP + wlo:SP + wlo + wn, :]
            z = jnp.zeros((8, C), jnp.float32)
            if i == 0:
                parts, m0 = [crow[s, b, 0], cm, cw, z], W
            elif i == NC - 1:
                parts, m0 = [cm, crow[s, b, 1], cw, z], 0
            else:
                parts, m0 = [cm, cw, z], 0
            h, c_next = update(gate, t, jnp.concatenate(parts, axis=0))
            c[b, i * M:(i + 1) * M, :] = c_next[m0:m0 + M]
            hf = h.astype(jnp.float32)
            main = hf[m0:m0 + M]
            stage[0, b, i * M:(i + 1) * M, :] = main.astype(jnp.bfloat16)
            hodd[b, PAD + i * RC:PAD + (i + 1) * RC, 8:8 + W, :] = main.reshape(RC, W, C)
            ring = hf[n * W:n * W + wn]
            f = flat(hodd, b)
            if i == 0:
                hodd[b, PAD - 1, 8:8 + W, :] = jnp.where(has[0], hf[:W], 0.0)
                f[strided(halo_w, PITCH), :] = jnp.where(has[0], ring[:RC], 0.0)
                f[strided(PAD * PITCH + halo_w, PITCH), :] = ring[RC:]
            elif i == NC - 1:
                hodd[b, PAD + H, 8:8 + W, :] = jnp.where(has[1], hf[M:M + W], 0.0)
                f[strided((PAD + i * RC) * PITCH + halo_w, PITCH), :] = ring[:RC]
                f[strided((PAD + H) * PITCH + halo_w, PITCH), :] = jnp.where(has[1], ring[RC:], 0.0)
            else:
                f[strided((PAD + i * RC) * PITCH + halo_w, PITCH), :] = ring

        return dot, epilogue

    def unit_b(n, b, i, t, send):
        def dot():
            parts = []
            for dh in range(3):
                for dw in range(3):
                    v = hodd[b, PAD + i * RC + dh - 1:PAD + (i + 1) * RC + dh - 1, 7 + dw:7 + dw + W, :]
                    parts.append(v.reshape(M, C).astype(jnp.bfloat16))
            return gates(parts, t)

        def epilogue(gate):
            h, c_next = update(gate, t, c[b, i * M:(i + 1) * M, :])
            c[b, i * M:(i + 1) * M, :] = c_next
            stage[1, b, i * M:(i + 1) * M, :] = h
            put(n, b, i, h.astype(jnp.float32).reshape(RC, W, C), c_next, send)

        return dot, epilogue

    def period(s, p, send):
        t = 2 * p
        n = 1 - s
        units = []
        for b in range(BATCH):
            seen = set()
            for i in A_ORDER:
                units.append((unit_a(s, b, i, t, seen), (0, b, t) if i == A_ORDER[-1] else None))
            for i in B_ORDER:
                units.append((unit_b(n, b, i, t + 1, send), (1, b, t + 1) if i == B_ORDER[-1] else None))
        held = None
        for unit in units + [None]:
            gate = unit[0][0]() if unit else None
            if held:
                (_, epilogue), out = held[0]
                epilogue(held[1])
                if out:
                    k, b, tt = out
                    out_copy(k, b, tt).start()
                    if k == 1:
                        out_copy(0, b, tt - 1).wait()
                        if b == 1:
                            out_copy(1, 0, tt).wait()
            held = (unit, gate) if unit else None

    c[...] = c0[...]
    for b in range(BATCH):
        for ref in (ha, hb, hodd):
            for at in (0, 8 + W):
                ref[b, :, at:at + 8, :] = jnp.zeros((ROWS, 8, C), jnp.float32)
    barrier = pltpu.get_barrier_semaphore()
    for dev in (dev_side,) + dev_row + dev_cor:
        pl.semaphore_signal(barrier, inc=1, device_id=dev, device_id_type=MESH)
    pl.semaphore_wait(barrier, 5)
    for b in range(BATCH):
        for i in range(NC):
            h = h0[b, i * M:(i + 1) * M, :].astype(jnp.float32).reshape(RC, W, C)
            put(0, b, i, h, c[b, i * M:(i + 1) * M, :], True)

    def two(q, _):
        @pl.when(q > 0)
        def _():
            out_copy(1, 1, 4 * q - 1).wait()
        period(0, 2 * q, True)
        out_copy(1, 1, 4 * q + 1).wait()
        period(1, 2 * q + 1, True)
        return 0

    lax.fori_loop(0, PERIODS // 2 - 1, two, 0)
    out_copy(1, 1, STEPS - 5).wait()
    period(0, PERIODS - 2, True)
    out_copy(1, 1, STEPS - 3).wait()
    period(1, PERIODS - 1, False)
    out_copy(1, 1, STEPS - 1).wait()


def solution(mesh):
    def device_fn(h_init, c_init, w_rec, gate_bias):
        cells = H * W
        vm = pl.BlockSpec(memory_space=pltpu.VMEM)
        tile = pltpu.VMEM((BATCH, ROWS, PITCH, C), jnp.float32)
        strip = pltpu.VMEM((BATCH, 6, SROWS, C), jnp.float32)
        pair_sems = pltpu.SemaphoreType.DMA((2, BATCH, 2))
        hseq, clast = pl.pallas_call(
            kernel,
            out_shape=(jax.ShapeDtypeStruct((STEPS, BATCH, cells, C), jnp.bfloat16),
                       jax.ShapeDtypeStruct((BATCH, cells, C), jnp.float32)),
            in_specs=[vm] * 4,
            out_specs=(pl.BlockSpec(memory_space=pl.ANY), vm),
            scratch_shapes=[
                tile, tile, tile, strip, strip,
                pltpu.VMEM((2, BATCH, 2, W, C), jnp.float32),
                pltpu.VMEM((2, BATCH, 2, 2, W, C), jnp.float32),
                pltpu.VMEM((2, BATCH, 2, W, C), jnp.float32),
                pltpu.VMEM((2, BATCH, 2, 3, RC, C), jnp.float32),
                pltpu.VMEM((2, BATCH, cells, C), jnp.bfloat16),
                pltpu.SemaphoreType.DMA((2, BATCH, NC)),
                pltpu.SemaphoreType.DMA((2, BATCH, NC)),
            ] + [pair_sems] * 8 + [pltpu.SemaphoreType.DMA((2, BATCH))],
            compiler_params=pltpu.CompilerParams(collective_id=0, has_side_effects=True, vmem_limit_bytes=48 << 20),
        )(h_init.reshape(BATCH, cells, C), c_init.reshape(BATCH, cells, C), w_rec.reshape(9 * C, 4 * C), gate_bias)
        return hseq.reshape(STEPS, BATCH, H, W, C), clast.reshape(BATCH, H, W, C)

    state_spec = P("dp", "rows", "cols", None)
    return jax.shard_map(device_fn, mesh=mesh, in_specs=(state_spec, state_spec, P(), P()),
                         out_specs=(P(None, "dp", "rows", "cols", None), state_spec), check_vma=False)
```

time: 542 us -> 112 us (0.21); the launches traced: 534 us -> 112 us
  starting transfers between devices: 287 us -> 0 us
  Pallas kernels: 0 us -> 96.1 us
  local copies, waits for them, and re-layouts: 96.7 us -> 15.3 us
  matrix products: 69.8 us -> 0 us
  other arithmetic: 40.1 us -> 0 us
  waiting for transfers between devices: 37.3 us -> 0 us
    ppermute x96 -> x0, starting transfers between devices: 287 us -> none  [the longest x24 116 us: with_halo(): from_above = lax.ppermute(tile[:, -1:], 'rows', rows_down)]
    pallas_call x0 -> x1, Pallas kernels: none -> 96.1 us  [device_fn(): pl.pallas_call(kernel, out_shape=(jax.ShapeDtypeStruct((STEPS, BATCH, cel...]
    conv_general_dilated x24 -> x0, matrix products: 69.8 us -> none  [one_step(): lax.conv_general_dilated(padded, w_rec, (1, 1), 'VALID', dimension_number...]
    ppermute x96 -> x0, waiting for transfers between devices: 37.3 us -> none  [the longest x24 19.7 us: with_halo(): from_above = lax.ppermute(tile[:, -1:], 'rows', rows_down)]
    div x48 -> x0, local copies, waits for them, and re-layouts: 29.4 us -> none  [lstm_update(): jax.nn.sigmoid(forget_gate) * c_prev]
    div x24 -> x0, other arithmetic: 22.9 us -> none  [lstm_update(): jax.nn.sigmoid(forget_gate) * c_prev]
    dynamic_update_slice x24 -> x0, local copies, waits for them, and re-layouts: 21.7 us -> none  [device_fn(): final_state, h_seq = lax.scan(one_step, (h_init, c_init), gate_bias)]
    dynamic_slice x24 -> x0, local copies, waits for them, and re-layouts: 17.5 us -> none  [device_fn(): final_state, h_seq = lax.scan(one_step, (h_init, c_init), gate_bias)]
  transfers between devices with their start and end apart: 96 -> 0, of which waited for: 48 -> 0; matrix products, arithmetic and copies ran while one was open for 3% -> 0% of each run, Pallas kernels for 0% -> 0%
where the time goes in v2:
time: 112 us
  Pallas kernels  96.1 us (86%)
  local copies, waits for them, and re-layouts  15.3 us (14%)
    pallas_call x1, Pallas kernels, device_fn(): pl.pallas_call(kernel, out_shape=(jax.ShapeDtypeStruct((STEPS, BATCH, cel...  96.1 us
    unnamed x10, local copies, waits for them, and re-layouts  15.3 us

profile of v2, /device:TPU:0, one launch (start us, length us, event | category | flops | bytes accessed | tf_op | source)
XLA Modules:
  0.0 112.1 jit_solution(3108996633018380789)
XLA Ops:
  0.6 0.0 copy-start
  0.6 1.3 %copy-done = bf16[3,3,128,512]{3,2,1,0:T(8,128)(2,1)S(1)} copy-done((bf16[3,3,128,512]{3,2,1,0:T(8,128)(2,1)S(1)}, bf16[3,3,128,512]{3,2,1,0:T(8,128)(2,1)}, u32[]{:S(2)}) %copy-start) | copy-done | bytes 1179672
  1.9 0.0 copy-start.1
  1.9 1.1 %copy-done.1 = f32[2,32,24,128]{3,2,1,0:T(8,128)S(1)} copy-done((f32[2,32,24,128]{3,2,1,0:T(8,128)S(1)}, f32[2,32,24,128]{3,2,1,0:T(8,128)}, u32[]{:S(2)}) %copy-start.1) | copy-done | bytes 786456
  3.0 0.0 copy-start.2
  3.0 1.0 copy-done.2
  4.0 0.0 copy-start.3
  4.0 0.8 copy-done.3
  4.8 96.1 %shard_map.59 = (bf16[24,2,768,128]{3,2,1,0:T(8,128)(2,1)}, f32[2,768,128]{2,1,0:T(8,128)S(1)}) custom-call(bf16[2,768,128]{2,1,0:T(8,128)(2,1)S(1)} %bitcast.8, f32[2,768,128]{2,1,0:T(8,128)S(1)} %bitcast.7, bf16[1152,512]{1,0:T(8,128)(2,1)S(1)} %bitcast.5, f32[24,512]{1,0:T(8,128)S(1)} %copy-done.3), custom_call_target="tpu_custom_call" | custom-call | tf_op jit(solution)/shard_map/pallas_call | solution.py:257
  101.0 10.3 %copy.8 = bf16[24,2,32,24,128]{4,3,2,1,0:T(8,128)(2,1)} copy(bf16[24,2,32,24,128]{4,3,2,1,0:T(8,128)(2,1)} %bitcast.9) | data formatting | bytes 18874368
  111.2 0.9 copy.9
Async XLA Ops:
  0.6 1.3 %copy-start = (bf16[3,3,128,512]{3,2,1,0:T(8,128)(2,1)S(1)}, bf16[3,3,128,512]{3,2,1,0:T(8,128)(2,1)}, u32[]{:S(2)}) copy-start(bf16[3,3,128,512]{3,2,1,0:T(8,128)(2,1)} %param.6) | copy-start | bytes 3538948
  1.9 1.1 %copy-start.1 = (f32[2,32,24,128]{3,2,1,0:T(8,128)S(1)}, f32[2,32,24,128]{3,2,1,0:T(8,128)}, u32[]{:S(2)}) copy-start(f32[2,32,24,128]{3,2,1,0:T(8,128)} %param.5) | copy-start | bytes 2359300
  3.0 1.0 copy-start.2
  4.0 0.8 copy-start.3

commit v3 on v2

--- a/solution.py
+++ b/solution.py
@@ -16,16 +16,17 @@
 ROWS = H + 2 * PAD
 SP = 16
 SROWS = H + 2 * SP
+PIECES = 12
 A_ORDER = (1, 2, 0, 3)
-B_ORDER = (1, 2, 0, 3)
+B_ORDER = (0, 3, 1, 2)
 
 
 def sigmoid(x):
     return 0.5 * jnp.tanh(0.5 * x) + 0.5
 
 
-def kernel(h0, c0, w, bias, hseq, c, ha, hb, hodd, sa, sb, crow, rsend, csend, ssend, stage,
-           s_col, r_col, s_row, r_row, s_crow, r_crow, s_own, r_own, s_cor, r_cor, s_out):
+def kernel(h0, c0, w, bias_in, hseq, c, ha, hb, hodd, sa, sb, crow, rsend, csend, ssend, wt, hin, bias,
+           s_col, r_col, s_row, r_row, s_crow, r_crow, s_own, r_own, s_cor, r_cor, s_w):
     he = (ha, hb)
     st = (sa, sb)
     row = lax.axis_index("rows")
@@ -68,9 +69,6 @@
 
     def strided(start, stride):
         return pl.ds(start, RC, stride)
-
-    def out_copy(k, b, t):
-        return pltpu.make_async_copy(stage.at[k, b], hseq.at[t, b], s_out.at[k, b])
 
     def put(s, b, i, h3, c2, send):
         he[s][b, PAD + i * RC:PAD + (i + 1) * RC, 8:8 + W, :] = h3
@@ -112,10 +110,11 @@
 
     def gates(parts, t):
         lhs = jnp.concatenate(parts, axis=1)
-        return jnp.dot(lhs, w[...], preferred_element_type=jnp.float32)
+        rhs = jnp.concatenate([wt[k] for k in range(4)], axis=1)
+        return jnp.dot(lhs, rhs, preferred_element_type=jnp.float32)
 
     def update(gate, t, c_prev):
-        gate = gate + bias[pl.ds(t, 1), :]
+        gate = bias[pl.ds(t, 1), :] + gate
         c_next = sigmoid(gate[:, C:2 * C]) * c_prev + sigmoid(gate[:, :C]) * jnp.tanh(gate[:, 3 * C:])
         return (sigmoid(gate[:, 2 * C:3 * C]) * jnp.tanh(c_next)).astype(jnp.bfloat16), c_next
 
@@ -126,14 +125,12 @@
         wn = RC * (2 if i in (0, NC - 1) else 1)
 
         def dot():
-            for j in range(max(i - 1, 0), min(i + 2, NC)):
-                if j not in seen:
-                    seen.add(j)
+            if not seen:
+                seen.add(i)
+                for j in range(NC):
                     take_col(s, b, j)
-            if i == 0:
-                take_row(s, b, 0)
-            if i == NC - 1:
-                take_row(s, b, 1)
+                for d in range(2):
+                    take_row(s, b, d)
             parts = []
             for dh in range(3):
                 for dw in range(3):
@@ -157,7 +154,7 @@
             c[b, i * M:(i + 1) * M, :] = c_next[m0:m0 + M]
             hf = h.astype(jnp.float32)
             main = hf[m0:m0 + M]
-            stage[0, b, i * M:(i + 1) * M, :] = main.astype(jnp.bfloat16)
+            hseq[t, b, i * M:(i + 1) * M, :] = main.astype(jnp.bfloat16)
             hodd[b, PAD + i * RC:PAD + (i + 1) * RC, 8:8 + W, :] = main.reshape(RC, W, C)
             ring = hf[n * W:n * W + wn]
             f = flat(hodd, b)
@@ -186,7 +183,7 @@
         def epilogue(gate):
             h, c_next = update(gate, t, c[b, i * M:(i + 1) * M, :])
             c[b, i * M:(i + 1) * M, :] = c_next
-            stage[1, b, i * M:(i + 1) * M, :] = h
+            hseq[t, b, i * M:(i + 1) * M, :] = h
             put(n, b, i, h.astype(jnp.float32).reshape(RC, W, C), c_next, send)
 
         return dot, epilogue
@@ -198,25 +195,23 @@
         for b in range(BATCH):
             seen = set()
             for i in A_ORDER:
-                units.append((unit_a(s, b, i, t, seen), (0, b, t) if i == A_ORDER[-1] else None))
+                units.append(unit_a(s, b, i, t, seen))
             for i in B_ORDER:
-                units.append((unit_b(n, b, i, t + 1, send), (1, b, t + 1) if i == B_ORDER[-1] else None))
-        held = None
-        for unit in units + [None]:
-            gate = unit[0][0]() if unit else None
-            if held:
-                (_, epilogue), out = held[0]
-                epilogue(held[1])
-                if out:
-                    k, b, tt = out
-                    out_copy(k, b, tt).start()
-                    if k == 1:
-                        out_copy(0, b, tt - 1).wait()
-                        if b == 1:
-                            out_copy(1, 0, tt).wait()
-            held = (unit, gate) if unit else None
-
-    c[...] = c0[...]
+                units.append(unit_b(n, b, i, t + 1, send))
+        half = len(units) // BATCH
+        for b in range(BATCH):
+            held = None
+            for unit in units[b * half:(b + 1) * half] + [None]:
+                gate = unit[0]() if unit else None
+                if held:
+                    held[0][1](held[1])
+                held = (unit, gate) if unit else None
+
+    load_state = [pltpu.make_async_copy(h0, hin, s_w.at[4]), pltpu.make_async_copy(c0, c, s_w.at[5])]
+    load_w = [pltpu.make_async_copy(w.at[:, k * C:(k + 1) * C], wt.at[k], s_w.at[k]) for k in range(4)]
+    load_w.append(pltpu.make_async_copy(bias_in, bias, s_w.at[6]))
+    for cp in load_state + load_w:
+        cp.start()
     for b in range(BATCH):
         for ref in (ha, hb, hodd):
             for at in (0, 8 + W):
@@ -224,33 +219,41 @@
     barrier = pltpu.get_barrier_semaphore()
     for dev in (dev_side,) + dev_row + dev_cor:
         pl.semaphore_signal(barrier, inc=1, device_id=dev, device_id_type=MESH)
+    for cp in load_state:
+        cp.wait()
     pl.semaphore_wait(barrier, 5)
     for b in range(BATCH):
         for i in range(NC):
-            h = h0[b, i * M:(i + 1) * M, :].astype(jnp.float32).reshape(RC, W, C)
+            h = hin[b, i * M:(i + 1) * M, :].astype(jnp.float32).reshape(RC, W, C)
             put(0, b, i, h, c[b, i * M:(i + 1) * M, :], True)
+    for cp in load_w:
+        cp.wait()
 
     def two(q, _):
-        @pl.when(q > 0)
-        def _():
-            out_copy(1, 1, 4 * q - 1).wait()
         period(0, 2 * q, True)
-        out_copy(1, 1, 4 * q + 1).wait()
         period(1, 2 * q + 1, True)
         return 0
 
     lax.fori_loop(0, PERIODS // 2 - 1, two, 0)
-    out_copy(1, 1, STEPS - 5).wait()
     period(0, PERIODS - 2, True)
-    out_copy(1, 1, STEPS - 3).wait()
     period(1, PERIODS - 1, False)
-    out_copy(1, 1, STEPS - 1).wait()
+
+
+def write_out(h, c, h_out, c_out, sems):
+    n = STEPS // PIECES
+    copies = [pltpu.make_async_copy(h.at[k * n:(k + 1) * n], h_out.at[k * n:(k + 1) * n], sems.at[k]) for k in range(PIECES)]
+    copies.append(pltpu.make_async_copy(c, c_out, sems.at[PIECES]))
+    for cp in copies:
+        cp.start()
+    for cp in copies:
+        cp.wait()
 
 
 def solution(mesh):
     def device_fn(h_init, c_init, w_rec, gate_bias):
         cells = H * W
         vm = pl.BlockSpec(memory_space=pltpu.VMEM)
+        hbm = pl.BlockSpec(memory_space=pltpu.HBM)
         tile = pltpu.VMEM((BATCH, ROWS, PITCH, C), jnp.float32)
         strip = pltpu.VMEM((BATCH, 6, SROWS, C), jnp.float32)
         pair_sems = pltpu.SemaphoreType.DMA((2, BATCH, 2))
@@ -258,20 +261,33 @@
             kernel,
             out_shape=(jax.ShapeDtypeStruct((STEPS, BATCH, cells, C), jnp.bfloat16),
                        jax.ShapeDtypeStruct((BATCH, cells, C), jnp.float32)),
-            in_specs=[vm] * 4,
-            out_specs=(pl.BlockSpec(memory_space=pl.ANY), vm),
+            in_specs=[hbm, hbm, hbm, hbm],
+            out_specs=(vm, vm),
             scratch_shapes=[
                 tile, tile, tile, strip, strip,
                 pltpu.VMEM((2, BATCH, 2, W, C), jnp.float32),
                 pltpu.VMEM((2, BATCH, 2, 2, W, C), jnp.float32),
                 pltpu.VMEM((2, BATCH, 2, W, C), jnp.float32),
                 pltpu.VMEM((2, BATCH, 2, 3, RC, C), jnp.float32),
-                pltpu.VMEM((2, BATCH, cells, C), jnp.bfloat16),
+                pltpu.VMEM((4, 9 * C, C), jnp.bfloat16),
+                pltpu.VMEM((BATCH, cells, C), jnp.bfloat16),
+                pltpu.VMEM((STEPS, 4 * C), jnp.float32),
                 pltpu.SemaphoreType.DMA((2, BATCH, NC)),
                 pltpu.SemaphoreType.DMA((2, BATCH, NC)),
-            ] + [pair_sems] * 8 + [pltpu.SemaphoreType.DMA((2, BATCH))],
-            compiler_params=pltpu.CompilerParams(collective_id=0, has_side_effects=True, vmem_limit_bytes=48 << 20),
-        )(h_init.reshape(BATCH, cells, C), c_init.reshape(BATCH, cells, C), w_rec.reshape(9 * C, 4 * C), gate_bias)
+            ] + [pair_sems] * 8 + [pltpu.SemaphoreType.DMA((7,))],
+            compiler_params=pltpu.CompilerParams(collective_id=0, has_side_effects=True, vmem_limit_bytes=26 << 20),
+        )(*(pltpu.with_memory_space_constraint(v, pltpu.HBM) for v in (
+            h_init.reshape(BATCH, cells, C), c_init.reshape(BATCH, cells, C), w_rec.reshape(9 * C, 4 * C), gate_bias)))
+        anywhere = pl.BlockSpec(memory_space=pl.ANY)
+        hseq, clast = pl.pallas_call(
+            write_out,
+            out_shape=(jax.ShapeDtypeStruct((STEPS, BATCH, cells, C), jnp.bfloat16),
+                       jax.ShapeDtypeStruct((BATCH, cells, C), jnp.float32)),
+            in_specs=[vm, vm],
+            out_specs=(anywhere, anywhere),
+            scratch_shapes=[pltpu.SemaphoreType.DMA((PIECES + 1,))],
+            compiler_params=pltpu.CompilerParams(vmem_limit_bytes=26 << 20),
+        )(hseq, clast)
         return hseq.reshape(STEPS, BATCH, H, W, C), clast.reshape(BATCH, H, W, C)
 
     state_spec = P("dp", "rows", "cols", None)

time: 112 us -> 79.4 us (0.71)
  Pallas kernels: 96.1 us -> 78.5 us
  local copies, waits for them, and re-layouts: 15.3 us -> 0 us
    pallas_call x1, Pallas kernels: 96.1 us -> 74.6 us  [device_fn(): pl.pallas_call(kernel, out_shape=(jax.ShapeDtypeStruct((STEPS, BATCH, cel...]
    unnamed x10 -> x0, local copies, waits for them, and re-layouts: 15.3 us -> none
    pallas_call x0 -> x1, Pallas kernels: none -> 3.97 us  [device_fn(): pl.pallas_call(write_out, out_shape=(jax.ShapeDtypeStruct((STEPS, BATCH,...]
where the time goes in v3:
time: 79.4 us; the launch traced here: 79.3 us
  Pallas kernels  78.5 us (99%)
  between operations  0.8 us (1%)
    pallas_call x1, Pallas kernels, device_fn(): pl.pallas_call(kernel, out_shape=(jax.ShapeDtypeStruct((STEPS, BATCH, cel...  74.6 us
    pallas_call x1, Pallas kernels, device_fn(): pl.pallas_call(write_out, out_shape=(jax.ShapeDtypeStruct((STEPS, BATCH,...  3.97 us

profile of v3, /device:TPU:0, one launch (start us, length us, event | category | flops | bytes accessed | tf_op | source)
XLA Modules:
  0.0 79.3 jit_solution(8633740497937073447)
XLA Ops:
  0.6 74.6 %shard_map.59 = (bf16[24,2,768,128]{3,2,1,0:T(8,128)(2,1)S(1)}, f32[2,768,128]{2,1,0:T(8,128)S(1)}) custom-call(bf16[2,768,128]{2,1,0:T(8,128)(2,1)} %bitcast.7, f32[2,768,128]{2,1,0:T(8,128)} %bitcast.6, bf16[1152,512]{1,0:T(8,128)(2,1)} %bitcast.5, f32[24,512]{1,0:T(8,128)} %bias_in.1), custom_call_target="tpu_custom_call" | custom-call | tf_op jit(solution)/shard_map/pallas_call | solution.py:260
  75.2 4.0 %shard_map.60 = (bf16[24,2,768,128]{3,2,1,0:T(8,128)(2,1)}, f32[2,768,128]{2,1,0:T(8,128)}) custom-call(bf16[24,2,768,128]{3,2,1,0:T(8,128)(2,1)S(1)} %get-tuple-element.6.h, f32[2,768,128]{2,1,0:T(8,128)S(1)} %get-tuple-element.7.c), custom_call_target="tpu_custom_call" | custom-call | tf_op jit(solution)/shard_map/pallas_call | solution.py:282

commit v4 on v3

--- a/solution.py
+++ b/solution.py
@@ -16,6 +16,8 @@
 ROWS = H + 2 * PAD
 SP = 16
 SROWS = H + 2 * SP
+PACK = 3 * W + 8
+CORNER = slice(3 * W, PACK)
 PIECES = 12
 A_ORDER = (1, 2, 0, 3)
 B_ORDER = (0, 3, 1, 2)
@@ -25,8 +27,8 @@
     return 0.5 * jnp.tanh(0.5 * x) + 0.5
 
 
-def kernel(h0, c0, w, bias_in, hseq, c, ha, hb, hodd, sa, sb, crow, rsend, csend, ssend, wt, hin, bias,
-           s_col, r_col, s_row, r_row, s_crow, r_crow, s_own, r_own, s_cor, r_cor, s_w):
+def kernel(h0, c0, w, bias_in, hseq, c, ha, hb, hodd, sa, sb, psend, precv, wt, hin, bias,
+           s_col, r_col, s_row, r_row, s_w):
     he = (ha, hb)
     st = (sa, sb)
     row = lax.axis_index("rows")
@@ -49,20 +51,15 @@
     def remote(src, dst, ssem, rsem, dev):
         return pltpu.make_async_remote_copy(src, dst, ssem, rsem, device_id=dev, device_id_type=MESH)
 
-    def col_copy(s, b, i):
-        rows = pl.ds(SP + i * RC, RC)
-        return [remote(st[s].at[b, 0:3, rows, :], st[s].at[b, 3:6, rows, :], s_col.at[s, b, i], r_col.at[s, b, i], dev_side)]
+    def col_copy(s, b, lo, n):
+        rows = pl.ds(SP + lo, n)
+        return remote(st[s].at[b, 0:3, rows, :], st[s].at[b, 3:6, rows, :], s_col.at[s, b], r_col.at[s, b], dev_side)
+
+    def row_copy(s, b, d, part, dev):
+        return remote(psend.at[s, b, d, part], precv.at[s, b, 1 - d, part], s_row.at[s, b, d], r_row.at[s, b, 1 - d], dev)
 
     def row_copies(s, b, d):
-        o = 1 - d
-        rows = pl.ds(PAD + H if d == 0 else PAD - 2, 2)
-        srows = pl.ds(SP + H if d == 0 else SP - RC, RC)
-        return [
-            remote(rsend.at[s, b, d], he[s].at[b, rows, 8:8 + W, :], s_row.at[s, b, d], r_row.at[s, b, o], dev_row[d]),
-            remote(csend.at[s, b, d], crow.at[s, b, o], s_crow.at[s, b, d], r_crow.at[s, b, o], dev_row[d]),
-            remote(ssend.at[s, b, d, 0:1], st[s].at[b, 0:1, srows, :], s_own.at[s, b, d], r_own.at[s, b, o], dev_row[d]),
-            remote(ssend.at[s, b, d], st[s].at[b, 3:6, srows, :], s_cor.at[s, b, d], r_cor.at[s, b, o], dev_cor[d]),
-        ]
+        return row_copy(s, b, d, CORNER, dev_cor[d]), row_copy(s, b, d, slice(0, 3 * W), dev_row[d])
 
     def flat(ref, b):
         return ref.at[b].reshape(ROWS * PITCH, C)
@@ -80,33 +77,38 @@
                  c.at[b][strided(i * M + edge_c, W), :])
         for k in range(3):
             st[s][b, k, SP + i * RC:SP + (i + 1) * RC, :] = strip[k]
-        col_copy(s, b, i)[0].start()
         for d in range(2):
             if i == (0 if d == 0 else NC - 1):
                 r = 0 if d == 0 else RC - 2
                 q = 0 if d == 0 else (RC - 1) * W
-                rsend[s, b, d] = jnp.where(has[d], h3[r:r + 2], 0.0)
-                csend[s, b, d] = jnp.where(has[d], c2[q:q + W], 0.0)
                 for k in range(3):
-                    ssend[s, b, d, k] = jnp.where(has[d], strip[k], 0.0)
+                    psend[s, b, d, 3 * W + 2 * k:3 * W + 2 * k + 2, :] = jnp.where(has[d], strip[k][r:r + 2], 0.0)
+                psend[s, b, d, 0:2 * W, :] = jnp.where(has[d], h3[r:r + 2].reshape(2 * W, C), 0.0)
+                psend[s, b, d, 2 * W:3 * W, :] = jnp.where(has[d], c2[q:q + W], 0.0)
                 for cp in row_copies(s, b, d):
                     cp.start()
+        col_copy(s, b, i * RC, RC).start()
 
     def insert(s, b, i):
         flat(he[s], b)[strided((PAD + i * RC) * PITCH + halo_w, PITCH), :] = st[s][b, 3, SP + i * RC:SP + (i + 1) * RC, :]
 
-    def take_col(s, b, i):
-        cp = col_copy(s, b, i)[0]
+    def take_cols(s, b):
+        cp = col_copy(s, b, 0, H)
         cp.wait_send()
         cp.wait_recv()
+        for i in range(NC):
+            insert(s, b, i)
+
+    def take_row(s, b, d):
+        row_copy(s, b, d, slice(0, PACK), dev_row[d]).wait_send()
+        row_copy(s, b, 1 - d, slice(0, PACK), dev_row[d]).wait_recv()
+        r = -2 if d == 0 else H
+        he[s][b, PAD + r:PAD + r + 2, 8:8 + W, :] = precv[s, b, d, 0:2 * W, :].reshape(2, W, C)
+        for k in range(3):
+            st[s][b, 3 + k, SP + r:SP + r + 2, :] = precv[s, b, d, 3 * W + 2 * k:3 * W + 2 * k + 2, :]
+        i = -1 if d == 0 else NC
         insert(s, b, i)
-
-    def take_row(s, b, d):
-        for cp in row_copies(s, b, d):
-            cp.wait_send()
-        for cp in row_copies(s, b, 1 - d):
-            cp.wait_recv()
-        insert(s, b, -1 if d == 0 else NC)
+        st[s][b, 0, SP + i * RC:SP + (i + 1) * RC, :] = flat(he[s], b)[strided((PAD + i * RC) * PITCH + edge_w, PITCH), :]
 
     def gates(parts, t):
         lhs = jnp.concatenate(parts, axis=1)
@@ -127,8 +129,7 @@
         def dot():
             if not seen:
                 seen.add(i)
-                for j in range(NC):
-                    take_col(s, b, j)
+                take_cols(s, b)
                 for d in range(2):
                     take_row(s, b, d)
             parts = []
@@ -145,9 +146,9 @@
             cw = st[s][b, 5, SP + wlo:SP + wlo + wn, :]
             z = jnp.zeros((8, C), jnp.float32)
             if i == 0:
-                parts, m0 = [crow[s, b, 0], cm, cw, z], W
+                parts, m0 = [precv[s, b, 0, 2 * W:3 * W, :], cm, cw, z], W
             elif i == NC - 1:
-                parts, m0 = [cm, crow[s, b, 1], cw, z], 0
+                parts, m0 = [cm, precv[s, b, 1, 2 * W:3 * W, :], cw, z], 0
             else:
                 parts, m0 = [cm, cw, z], 0
             h, c_next = update(gate, t, jnp.concatenate(parts, axis=0))
@@ -256,6 +257,7 @@
         hbm = pl.BlockSpec(memory_space=pltpu.HBM)
         tile = pltpu.VMEM((BATCH, ROWS, PITCH, C), jnp.float32)
         strip = pltpu.VMEM((BATCH, 6, SROWS, C), jnp.float32)
+        pack = pltpu.VMEM((2, BATCH, 2, PACK, C), jnp.float32)
         pair_sems = pltpu.SemaphoreType.DMA((2, BATCH, 2))
         hseq, clast = pl.pallas_call(
             kernel,
@@ -265,16 +267,16 @@
             out_specs=(vm, vm),
             scratch_shapes=[
                 tile, tile, tile, strip, strip,
-                pltpu.VMEM((2, BATCH, 2, W, C), jnp.float32),
-                pltpu.VMEM((2, BATCH, 2, 2, W, C), jnp.float32),
-                pltpu.VMEM((2, BATCH, 2, W, C), jnp.float32),
-                pltpu.VMEM((2, BATCH, 2, 3, RC, C), jnp.float32),
+                pack, pack,
                 pltpu.VMEM((4, 9 * C, C), jnp.bfloat16),
                 pltpu.VMEM((BATCH, cells, C), jnp.bfloat16),
                 pltpu.VMEM((STEPS, 4 * C), jnp.float32),
-                pltpu.SemaphoreType.DMA((2, BATCH, NC)),
-                pltpu.SemaphoreType.DMA((2, BATCH, NC)),
-            ] + [pair_sems] * 8 + [pltpu.SemaphoreType.DMA((7,))],
+                pltpu.SemaphoreType.DMA((2, BATCH)),
+                pltpu.SemaphoreType.DMA((2, BATCH)),
+                pair_sems,
+                pair_sems,
+                pltpu.SemaphoreType.DMA((7,)),
+            ],
             compiler_params=pltpu.CompilerParams(collective_id=0, has_side_effects=True, vmem_limit_bytes=26 << 20),
         )(*(pltpu.with_memory_space_constraint(v, pltpu.HBM) for v in (
             h_init.reshape(BATCH, cells, C), c_init.reshape(BATCH, cells, C), w_rec.reshape(9 * C, 4 * C), gate_bias)))

time: 79.4 us -> 77.9 us (0.981)
  Pallas kernels: 78.5 us -> 77 us
    pallas_call x1, Pallas kernels: 74.6 us -> 73 us  [device_fn(): pl.pallas_call(kernel, out_shape=(jax.ShapeDtypeStruct((STEPS, BATCH, cel...]
where the time goes in v4:
time: 77.9 us; the launch traced here: 77.8 us
  Pallas kernels  77 us (99%)
  between operations  0.8 us (1%)
    pallas_call x1, Pallas kernels, device_fn(): pl.pallas_call(kernel, out_shape=(jax.ShapeDtypeStruct((STEPS, BATCH, cel...  73 us
    pallas_call x1, Pallas kernels, device_fn(): pl.pallas_call(write_out, out_shape=(jax.ShapeDtypeStruct((STEPS, BATCH,...  3.97 us

profile of v4, /device:TPU:0, one launch (start us, length us, event | category | flops | bytes accessed | tf_op | source)
XLA Modules:
  0.0 77.8 jit_solution(8634394543285202777)
XLA Ops:
  0.6 73.0 %shard_map.59 = (bf16[24,2,768,128]{3,2,1,0:T(8,128)(2,1)S(1)}, f32[2,768,128]{2,1,0:T(8,128)S(1)}) custom-call(bf16[2,768,128]{2,1,0:T(8,128)(2,1)} %bitcast.7, f32[2,768,128]{2,1,0:T(8,128)} %bitcast.6, bf16[1152,512]{1,0:T(8,128)(2,1)} %bitcast.5, f32[24,512]{1,0:T(8,128)} %bias_in.1), custom_call_target="tpu_custom_call" | custom-call | tf_op jit(solution)/shard_map/pallas_call | solution.py:262
  73.7 4.0 %shard_map.60 = (bf16[24,2,768,128]{3,2,1,0:T(8,128)(2,1)}, f32[2,768,128]{2,1,0:T(8,128)}) custom-call(bf16[24,2,768,128]{3,2,1,0:T(8,128)(2,1)S(1)} %get-tuple-element.6.h, f32[2,768,128]{2,1,0:T(8,128)S(1)} %get-tuple-element.7.c), custom_call_target="tpu_custom_call" | custom-call | tf_op jit(solution)/shard_map/pallas_call | solution.py:284
